TPU v7x, 32 devices: a whole 2x2x4 slice. The times are simulated.
32 devices in a mesh: dp: 4 (over z), tp: 8 (over y, x, core).
Axes of the slice: x: 2, y: 2, z: 4, core: 2. Of those that a mesh axis runs over, the one named last changes fastest.
Arguments:
- resid_in: bfloat16 [512, 6144], P('dp'), parts along dimension 0
- positions: int32 [512], P('dp'), parts along dimension 0
- k_cache: bfloat16 [512, 128, 8, 128], P('dp', None, 'tp'), parts along dimension 0
- v_cache: bfloat16 [512, 128, 8, 128], P('dp', None, 'tp'), parts along dimension 0
- gain_attn: bfloat16 [6144], replicated
- w_query: bfloat16 [6144, 6144], P(None, 'tp')
- w_key: bfloat16 [6144, 1024], P(None, 'tp')
- w_value: bfloat16 [6144, 1024], P(None, 'tp')
- w_out: bfloat16 [6144, 6144], P('tp')
- gain_mlp: bfloat16 [6144], replicated
- w_gate: bfloat16 [6144, 16384], P(None, 'tp')
- w_up: bfloat16 [6144, 16384], P(None, 'tp')
- w_down: bfloat16 [16384, 6144], P('tp')
Outputs:
- output 1: bfloat16 [512, 6144], P('dp'), parts along dimension 0
- output 2: bfloat16 [512, 128, 8, 128], P('dp', None, 'tp'), parts along dimension 0
- output 3: bfloat16 [512, 128, 8, 128], P('dp', None, 'tp'), parts along dimension 0
There are 4 independent parts. A program takes and returns all parts, laid end to end along the dimension named above; an argument that names none is the same for every part.
All inputs are finite; a program needn't handle non-finite values.
Results may differ from a plain program's by a relative error of at most 0.0104617.
Values sent between devices are 32-bit elements.
A program may use at most 1 GiB of HBM per device.

v0:
```python
import math
import jax
import jax.numpy as jnp
from jax import lax
from jax.sharding import PartitionSpec as P

EPS = 1e-5
ROPE_THETA = 500000.0
ROPE_FACTOR = 8.0
LOW_FACTOR = 1.0
HIGH_FACTOR = 4.0
ORIG_CTX = 8192.0


def rms_norm(rows_in, gain):
    rows_f = rows_in.astype(jnp.float32)
    mean_sq = jnp.mean(rows_f * rows_f, axis=-1, keepdims=True)
    return (rows_f * lax.rsqrt(mean_sq + EPS) * gain.astype(jnp.float32)).astype(jnp.bfloat16)


def rope_tables(positions, head_dim):
    half_dim = head_dim // 2
    exponents = jnp.arange(half_dim, dtype=jnp.float32) * (2.0 / head_dim)
    inv_freq = 1.0 / jnp.power(ROPE_THETA, exponents)
    wavelen = (2.0 * math.pi) / inv_freq
    smooth = (ORIG_CTX / wavelen - LOW_FACTOR) / (HIGH_FACTOR - LOW_FACTOR)
    blended = (1.0 - smooth) * inv_freq / ROPE_FACTOR + smooth * inv_freq
    inv_freq = jnp.where(wavelen < ORIG_CTX / HIGH_FACTOR, inv_freq,
                         jnp.where(wavelen > ORIG_CTX / LOW_FACTOR, inv_freq / ROPE_FACTOR, blended))
    angles = positions.astype(jnp.float32)[:, None] * inv_freq[None, :]
    return jnp.cos(angles), jnp.sin(angles)


def apply_rope(vectors, cos_t, sin_t):
    half_dim = vectors.shape[-1] // 2
    lower_half = vectors[..., :half_dim]
    upper_half = vectors[..., half_dim:]
    cos_b = cos_t[:, None, :]
    sin_b = sin_t[:, None, :]
    return jnp.concatenate([lower_half * cos_b - upper_half * sin_b,
                            upper_half * cos_b + lower_half * sin_b], axis=-1)


def attention_block(resid_in, positions, k_cache, v_cache, gain_attn, w_query, w_key, w_value):
    n_seqs = resid_in.shape[0]
    cache_len = k_cache.shape[1]
    kv_heads = k_cache.shape[2]
    head_dim = k_cache.shape[3]
    group_size = w_query.shape[1] // (kv_heads * head_dim)
    normed = rms_norm(resid_in, gain_attn)
    queries = jnp.dot(normed, w_query, preferred_element_type=jnp.float32).astype(jnp.bfloat16)
    key_new = jnp.dot(normed, w_key, preferred_element_type=jnp.float32).astype(jnp.bfloat16)
    value_new = jnp.dot(normed, w_value, preferred_element_type=jnp.float32).astype(jnp.bfloat16)
    cos_t, sin_t = rope_tables(positions, head_dim)
    queries = apply_rope(queries.reshape(n_seqs, kv_heads * group_size, head_dim).astype(jnp.float32), cos_t, sin_t)
    queries = queries.astype(jnp.bfloat16).reshape(n_seqs, kv_heads, group_size, head_dim)
    key_new = apply_rope(key_new.reshape(n_seqs, kv_heads, head_dim).astype(jnp.float32), cos_t, sin_t)
    key_new = key_new.astype(jnp.bfloat16)
    value_new = value_new.reshape(n_seqs, kv_heads, head_dim)
    slot_iota = lax.broadcasted_iota(jnp.int32, (n_seqs, cache_len), 1)
    slot_hit = (slot_iota == positions[:, None])[:, :, None, None]
    k_full = jnp.where(slot_hit, key_new[:, None], k_cache)
    v_full = jnp.where(slot_hit, value_new[:, None], v_cache)
    scores = jnp.einsum('bkgd,bskd->bkgs', queries, k_full, preferred_element_type=jnp.float32)
    scores = scores * (1.0 / math.sqrt(head_dim))
    valid = (slot_iota <= positions[:, None])[:, None, None, :]
    scores = jnp.where(valid, scores, -jnp.inf)
    attn_prob = jax.nn.softmax(scores, axis=-1).astype(jnp.bfloat16)
    attn_out = jnp.einsum('bkgs,bskd->bkgd', attn_prob, v_full, preferred_element_type=jnp.float32)
    attn_out = attn_out.astype(jnp.bfloat16).reshape(n_seqs, kv_heads * group_size * head_dim)
    return attn_out, k_full, v_full


def gated_hidden(normed, w_gate, w_up):
    gate_proj = jnp.dot(normed, w_gate, preferred_element_type=jnp.float32).astype(jnp.bfloat16)
    up_proj = jnp.dot(normed, w_up, preferred_element_type=jnp.float32).astype(jnp.bfloat16)
    return (jax.nn.silu(gate_proj.astype(jnp.float32)) * up_proj.astype(jnp.float32)).astype(jnp.bfloat16)


def solution(mesh):
    def layer_local(resid_in, positions, k_cache, v_cache, gain_attn, w_query, w_key, w_value,
                    w_out, gain_mlp, w_gate, w_up, w_down):
        attn_out, k_full, v_full = attention_block(resid_in, positions, k_cache, v_cache,
                                                   gain_attn, w_query, w_key, w_value)
        y_part = jnp.dot(attn_out, w_out, preferred_element_type=jnp.float32)
        y_sum = lax.psum(y_part, 'tp')
        resid_mid = (resid_in.astype(jnp.float32) + y_sum).astype(jnp.bfloat16)
        hidden = gated_hidden(rms_norm(resid_mid, gain_mlp), w_gate, w_up)
        z_part = jnp.dot(hidden, w_down, preferred_element_type=jnp.float32)
        z_sum = lax.psum(z_part, 'tp')
        resid_out = (resid_mid.astype(jnp.float32) + z_sum).astype(jnp.bfloat16)
        return resid_out, k_full, v_full

    row_spec = P('dp', None)
    cache_spec = P('dp', None, 'tp', None)
    col_spec = P(None, 'tp')
    split_rows = P('tp', None)
    return jax.shard_map(layer_local, mesh=mesh,
                         in_specs=(row_spec, P('dp'), cache_spec, cache_spec, P(), col_spec, col_spec,
                                   col_spec, split_rows, P(), col_spec, col_spec, split_rows),
                         out_specs=(row_spec, cache_spec, cache_spec), check_vma=False)
```

profile of v0, /device:TPU:0, one launch (start us, length us, event | category | flops | bytes accessed | tf_op | source)
XLA Modules:
  0.0 230.4 jit_solution(17567770868204400301)
XLA Ops:
  7.2 0.0 copy-start
  7.2 0.0 copy-start.3
  7.2 0.0 all-reduce.3.cloned.1.call-start
  7.2 0.0 copy-start.6
  7.3 0.8 convert_element_type.89
  8.1 1.2 iota_compare_fusion.1
  9.3 1.8 fusion.5
  11.1 0.7 convert_element_type.84
  11.8 0.0 copy-done
  11.8 2.1 convolution_convert_fusion.3
  13.9 0.0 copy-done.3
  13.9 0.0 copy-done.6
  13.9 0.8 fusion.31
  14.8 0.3 multiply_cosine_fusion
  15.1 0.2 fusion.54
  15.3 0.1 copy.20
  15.4 5.1 %fusion.29 = f32[128,768]{1,0:T(8,128)S(1)} fusion(bf16[6144,768]{1,0:T(8,128)(2,1)} %param.18, bf16[128,6144]{1,0:T(8,128)(2,1)S(1)} %copy-done.3, f32[6144]{0:T(1024)S(1)} %convert_element_type.84, f32[128]{0:T(128)S(1)} %add_rsqrt_fusion.1), kind=kOutput, calls=%fused_computation.34 | convolution fusion | flops 1211301888 | bytes 11428352 | tf_op jit(solution)/shard_map/dot_general | solution.py:51
  20.5 0.2 copy.17
  20.7 0.2 copy.23
  21.0 0.2 copy.22
  21.2 0.1 subtract_convert_fusion
  21.4 8.5 %broadcast_select_fusion.1 = (bf16[128,128,1,128]{3,1,2,0:T(8,128)(2,1)S(1)}, bf16[128,128,1,128]{3,1,2,0:T(8,128)(2,1)}) fusion(bf16[128,128,1,128]{3,1,2,0:T(8,128)(2,1)} %param.15, pred[128,128]{1,0:T(8,128)(4,1)S(1)} %get-tuple-element.16, bf16[128,128]{1,0:T(8,128)(2,1)S(1)} %copy.20, bf16[128,128,1,128]{3,1,2,0:T(8,128)(2,1)} %param.16, ...), kind=kLoop, calls=%fused_computation.12 | loop fusion | flops 4194304 | bytes 16859136 | tf_op jit(solution)/shard_map/jit(_where)/select_n | solution.py:62
  29.9 0.0 copy-start.2
  29.9 2.0 copy-done.2
  31.9 2.3 fusion.23
  34.2 0.4 fusion.62
  34.6 4.0 %fusion.26 = bf16[128,6,128]{2,1,0:T(8,128)(2,1)S(1)} fusion(bf16[128,128,1,128]{3,1,2,0:T(8,128)(2,1)} %get-tuple-element.12, f32[128,6]{1,0:T(8,128)S(1)} %fusion.62, f32[128,6,128]{2,1,0:T(8,128)S(1)} %fusion.23), kind=kOutput, calls=%fused_computation.32 | convolution fusion | flops 25559936 | bytes 4787200 | tf_op jit(solution)/shard_map/bkgs,bskd->bkgd/dot_general | solution.py:69
  38.6 0.2 copy.21
  38.8 6.8 %fusion.63 = f32[128,6144]{1,0:T(8,128)} fusion(bf16[128,768]{0,1:T(8,128)(2,1)S(1)} %bitcast.34, bf16[768,6144]{1,0:T(8,128)(2,1)} %param.21), kind=kOutput, calls=%fused_computation.77 | convolution fusion | flops 1207959552 | bytes 12779520 | tf_op jit(solution)/shard_map/dot_general | solution.py:85
  45.6 0.0 copy-start.5
  45.6 0.0 copy-start.4
  45.6 0.0 all-reduce.3.cloned.1.call-update
  45.7 0.2 all-reduce.5.cloned.1.call-start
  45.9 0.4 copy-done.5
  46.3 71.4 %all-reduce.3.cloned.1.call-done = f32[128,6144]{1,0:T(8,128)} async-done(((f32[128,6144]{1,0:T(8,128)}), f32[128,6144]{1,0:T(8,128)}) %all-reduce.3.cloned.1.call-update) | async-done | bytes 3145744 | tf_op jit(solution)/shard_map/psum | solution.py:86
  117.7 0.0 copy-done.4
  117.7 2.4 %fusion.9 = (f32[128]{0:T(128)S(1)}, bf16[128,6144]{1,0:T(8,128)(2,1)S(1)}) fusion(f32[128,6144]{1,0:T(8,128)} %all-reduce.3.cloned.1.call-done, bf16[128,6144]{1,0:T(8,128)(2,1)S(1)} %copy-done.4), kind=kLoop, calls=%fused_computation.17 | loop fusion | flops 4718464 | bytes 6291968 | tf_op jit(solution)/shard_map/reduce_sum | solution.py:17
  120.2 10.0 %fusion.17 = f32[128,2048]{1,0:T(8,128)S(1)} fusion(bf16[6144,2048]{1,0:T(8,128)(2,1)} %param.23, bf16[128,6144]{1,0:T(8,128)(2,1)S(1)} %get-tuple-element.4, f32[6144]{0:T(1024)S(1)} %convert_element_type.98, f32[128]{0:T(128)S(1)} %add_rsqrt_fusion), kind=kOutput, calls=%fused_computation.27 | convolution fusion | flops 3224895488 | bytes 27812352 | tf_op jit(solution)/shard_map/dot_general | solution.py:75
  130.2 20.6 %fusion.16 = f32[128,6144]{1,0:T(8,128)} fusion(bf16[2048,6144]{1,0:T(8,128)(2,1)} %param.25, bf16[6144,2048]{1,0:T(8,128)(2,1)} %param.24, f32[128,2048]{1,0:T(8,128)S(1)} %fusion.17, bf16[128,6144]{1,0:T(8,128)(2,1)S(1)} %get-tuple-element.4, f32[6144]{0:T(1024)S(1)} %convert_element_type.98, f32[128]{0:T(128)S(1)} %add_rsqrt_fusion), kind=kOutput, calls=%fused_computation.25 | convolution fusion | flops 6447693824 | bytes 56123904 | tf_op jit(solution)/shard_map/dot_general | solution.py:89
  150.9 0.0 all-reduce.5.cloned.1.call-update
  150.9 0.0 copy-start.1
  150.9 69.3 %all-reduce.5.cloned.1.call-done = f32[128,6144]{1,0:T(8,128)} async-done(((f32[128,6144]{1,0:T(8,128)}), f32[128,6144]{1,0:T(8,128)}) %all-reduce.5.cloned.1.call-update) | async-done | bytes 3145744 | tf_op jit(solution)/shard_map/psum | solution.py:90
  220.2 3.3 %fusion.12 = bf16[128,6144]{1,0:T(8,128)(2,1)} fusion(f32[128,6144]{1,0:T(8,128)} %all-reduce.5.cloned.1.call-done, bf16[128,6144]{1,0:T(8,128)(2,1)S(1)} %get-tuple-element.4), kind=kLoop, calls=%fused_computation.20 | loop fusion | flops 2359296 | bytes 6291456 | tf_op jit(solution)/shard_map/convert_element_type | solution.py:91
  223.5 0.0 copy-done.1
  (6 shorter events, 0.1 us)
Async XLA Ops:
  7.2 4.7 %copy-start = (bf16[6144,128]{1,0:T(8,128)(2,1)S(1)}, bf16[6144,128]{1,0:T(8,128)(2,1)}, u32[]{:S(2)}) copy-start(bf16[6144,128]{1,0:T(8,128)(2,1)} %param.20) | copy-start | bytes 4718596
  7.2 6.7 %copy-start.3 = (bf16[128,6144]{1,0:T(8,128)(2,1)S(1)}, bf16[128,6144]{1,0:T(8,128)(2,1)}, u32[]{:S(2)}) copy-start(bf16[128,6144]{1,0:T(8,128)(2,1)} %param.13) | copy-start | bytes 4718596
  7.2 110.5 %all-reduce.3.cloned.1.call-start = ((), (), s32[]{:S(2)}) async-start(), calls=%async_computation | async-start | bytes 6291456 | tf_op jit(solution)/shard_map/psum | solution.py:86
  7.2 6.6 %copy-start.6 = (bf16[6144,128]{1,0:T(8,128)(2,1)S(1)}, bf16[6144,128]{1,0:T(8,128)(2,1)}, u32[]{:S(2)}) copy-start(bf16[6144,128]{1,0:T(8,128)(2,1)} %param.19) | copy-start | bytes 4718596
  29.9 2.0 copy-start.2
  45.6 0.7 copy-start.5
  45.6 72.1 %copy-start.4 = (bf16[128,6144]{1,0:T(8,128)(2,1)S(1)}, bf16[128,6144]{1,0:T(8,128)(2,1)}, u32[]{:S(2)}) copy-start(bf16[128,6144]{1,0:T(8,128)(2,1)} %param.13) | copy-start | bytes 4718596
  45.7 174.5 %all-reduce.5.cloned.1.call-start = ((), (), s32[]{:S(2)}) async-start(), calls=%async_computation.1 | async-start | bytes 6291456 | tf_op jit(solution)/shard_map/psum | solution.py:90
  150.9 72.7 %copy-start.1 = (bf16[6144,128]{1,0:T(8,128)(2,1)S(1)}, bf16[6144,128]{1,0:T(8,128)(2,1)}, u32[]{:S(2)}) copy-start(bf16[6144,128]{1,0:T(8,128)(2,1)} %param.20) | copy-start | bytes 4718596
Sparse Core Ops, SparseCore 0:
  45.8 71.9 all-reduce.2
  151.0 69.1 all-reduce.4
where the time goes:
time: 231 us; the launch traced here: 230 us
  waiting for transfers between devices  141 us (61%)
  matrix products  51.8 us (22%)
  other arithmetic  19.9 us (9%)
  between operations  14.2 us (6%)
  local copies, waits for them, and re-layouts  3.48 us (2%)
    psum x1, waiting for transfers between devices, layer_local(): y_sum = lax.psum(y_part, 'tp')  71.4 us
    psum x1, waiting for transfers between devices, layer_local(): z_sum = lax.psum(z_part, 'tp')  69.3 us
    dot_general x1, matrix products, layer_local(): z_part = jnp.dot(hidden, w_down, preferred_element_type=jnp.float32)  20.6 us
    dot_general x1, matrix products, gated_hidden(): jnp.dot(normed, w_gate, preferred_element_type=jnp.float32)  10 us
    select_n x1, other arithmetic, attention_block(): k_full = jnp.where(slot_hit, key_new[:, None], k_cache)  8.49 us
    dot_general x1, matrix products, layer_local(): y_part = jnp.dot(attn_out, w_out, preferred_element_type=jnp.float32)  6.84 us
    dot_general x1, matrix products, attention_block(): jnp.dot(normed, w_query, preferred_element_type=jnp.float32)  5.13 us
  transfers between devices with their start and end apart: 2, of which 2 were waited for; matrix products, arithmetic and copies ran while one was open for 0% of the time, Pallas kernels for 0%

commit v1 on v0

--- a/solution.py
+++ b/solution.py
@@ -2,6 +2,8 @@
 import jax
 import jax.numpy as jnp
 from jax import lax
+from jax.experimental import pallas as pl
+from jax.experimental.pallas import tpu as pltpu
 from jax.sharding import PartitionSpec as P
 
 EPS = 1e-5
@@ -71,10 +73,375 @@
     return attn_out, k_full, v_full
 
 
-def gated_hidden(normed, w_gate, w_up):
-    gate_proj = jnp.dot(normed, w_gate, preferred_element_type=jnp.float32).astype(jnp.bfloat16)
-    up_proj = jnp.dot(normed, w_up, preferred_element_type=jnp.float32).astype(jnp.bfloat16)
-    return (jax.nn.silu(gate_proj.astype(jnp.float32)) * up_proj.astype(jnp.float32)).astype(jnp.bfloat16)
+F32 = jnp.float32
+BF16 = jnp.bfloat16
+REL = ((1, 1), (0, 1), (1, 0), (0, 0))
+WO_SLOTS = 4
+GU_SLOTS = 5
+WD_SLOTS = 4
+GATHER_ORDER = ((0, 3), (1, 3), (0, 1), (0, 2), (1, 1), (1, 2), (0, 0), (1, 0))
+
+
+def flip(coord, do_flip):
+    return 1 - coord if do_flip else coord
+
+
+def tail_kernel(attn_ref, gain_ref, resid_hbm, wo_hbm, wg_hbm, wu_hbm, wd_hbm, out_hbm,
+                wo_buf, wg_buf, wu_buf, wd_buf, ybuf, dbuf, r1, r2, xg, acc_g, acc_u, abuf, hbuf,
+                resid_buf, obuf, stat, stat_out, gbuf, rbuf,
+                wo_sem, gu_sem, wd_sem, resid_sem, out_sem, d_send, d_recv, rs_send, rs_recv,
+                ag_send, ag_recv, st_send, st_recv):
+    rows = attn_ref.shape[0]
+    half = rows // 2
+    block = wo_buf.shape[2]
+    piece = block // 2
+    width = 8 * block
+
+    tp = lax.axis_index('tp')
+    core = tp % 2
+    x_pos = (tp // 2) % 2
+    y_pos = tp // 4
+
+    def device(flip_core, rel):
+        flip_y, flip_x = rel
+        return flip(y_pos, flip_y) * 4 + flip(x_pos, flip_x) * 2 + flip(core, flip_core)
+
+    def owner(flip_core, e):
+        return device(flip_core, REL[e])
+
+    def cols(o):
+        return pl.ds(pl.multiple_of(o * block, block), block)
+
+    me = owner(0, 3)
+    dev_d = owner(1, 3)
+    dev_x = owner(0, 1)
+    dev_y = owner(0, 2)
+
+    def remote(src, dst, send, recv, dev):
+        return pltpu.make_async_remote_copy(src_ref=src, dst_ref=dst, send_sem=send, recv_sem=recv,
+                                            device_id={'tp': dev}, device_id_type=pl.DeviceIdType.MESH)
+
+    order_cols = [(1 - t % 2, t // 2) for t in range(8)]
+
+    def wo_copy(t):
+        o = owner(*order_cols[t])
+        return pltpu.make_async_copy(wo_hbm.at[:, cols(o)], wo_buf.at[t % WO_SLOTS], wo_sem.at[t % WO_SLOTS])
+
+    def gu_copies(k):
+        o = owner(*GATHER_ORDER[k])
+        s = k % GU_SLOTS
+        return (pltpu.make_async_copy(wg_hbm.at[cols(o), :], wg_buf.at[s], gu_sem.at[0, s]),
+                pltpu.make_async_copy(wu_hbm.at[cols(o), :], wu_buf.at[s], gu_sem.at[1, s]))
+
+    def wd_copy(t):
+        o = owner(*order_cols[t])
+        return pltpu.make_async_copy(wd_hbm.at[:, cols(o)], wd_buf.at[t % WD_SLOTS], wd_sem.at[t % WD_SLOTS])
+
+    for t in range(WO_SLOTS):
+        wo_copy(t).start()
+    resid_copy = pltpu.make_async_copy(resid_hbm.at[:, cols(me)], resid_buf, resid_sem)
+    resid_copy.start()
+
+    barrier = pltpu.get_barrier_semaphore()
+    for j in range(1, 8):
+        pl.semaphore_signal(barrier, inc=1, device_id={'tp': (tp + j) % 8}, device_id_type=pl.DeviceIdType.MESH)
+
+    for o in range(8):
+        gbuf[o] = gain_ref[:, o * block:(o + 1) * block].astype(F32)
+
+    def store_block(dc, e, res):
+        for h in range(2):
+            for ab in range(2):
+                ybuf[dc, e, h, ab] = res[h * half:(h + 1) * half, ab * piece:(ab + 1) * piece]
+
+    def d2d(e):
+        return remote(ybuf.at[1, e], dbuf.at[e], d_send.at[e], d_recv.at[e], dev_d)
+
+    def rs_copy(m, h):
+        src, dst, dev = (
+            (ybuf.at[0, 0, h, 0], r1.at[0, 0, h], dev_x),
+            (ybuf.at[0, 1, h, 0], r1.at[0, 1, h], dev_x),
+            (ybuf.at[0, 1, h, 1], r2.at[1, h], dev_x),
+            (ybuf.at[0, 0, h, 1], r1.at[1, 0, h], dev_y),
+            (ybuf.at[0, 2, h, 1], r1.at[1, 1, h], dev_y),
+            (ybuf.at[0, 2, h, 0], r2.at[0, h], dev_y),
+        )[m]
+        return remote(src, dst, rs_send.at[m, h], rs_recv.at[m, h], dev)
+
+    def add_partner(e):
+        d2d(e).wait_recv()
+        for h in range(2):
+            for ab in range(2):
+                ybuf[0, e, h, ab] = ybuf[0, e, h, ab] + dbuf[e, h, ab]
+            if e == 0:
+                rs_copy(0, h).start()
+                rs_copy(3, h).start()
+            if e == 1:
+                rs_copy(1, h).start()
+            if e == 2:
+                rs_copy(4, h).start()
+
+    def ag_copy(m, h):
+        ox, oy, oxy = owner(0, 1), owner(0, 2), owner(0, 0)
+        ref, dev = (
+            (xg.at[me, h], dev_x),
+            (xg.at[me, h], dev_y),
+            (xg.at[me, h], dev_d),
+            (xg.at[oy, h, 0], dev_x),
+            (xg.at[ox, h, 1], dev_y),
+            (xg.at[ox, h], dev_d),
+            (xg.at[oy, h], dev_d),
+            (xg.at[oxy, h, 0], dev_d),
+            (xg.at[oxy, h, 1], dev_d),
+        )[m]
+        return remote(ref, ref, ag_send.at[m, h], ag_recv.at[m, h], dev)
+
+    def reduce_scatter_rest(first_half_terms):
+        for h in range(2):
+            rs_copy(3, h).wait_recv()
+            ybuf[0, 1, h, 1] = ybuf[0, 1, h, 1] + r1[1, 0, h]
+            rs_copy(2, h).start()
+            rs_copy(0, h).wait_recv()
+            ybuf[0, 2, h, 0] = ybuf[0, 2, h, 0] + r1[0, 0, h]
+            rs_copy(5, h).start()
+        for h in range(2):
+            rs_copy(1, h).wait_recv()
+            rs_copy(4, h).wait_recv()
+            rs_copy(2, h).wait_recv()
+            rs_copy(5, h).wait_recv()
+            for ab in range(2):
+                total = ybuf[0, 3, h, ab] + r1[ab, 1, h] + r2[ab, h]
+                xg[me, h, ab] = (first_half_terms(h, ab) + total).astype(BF16).astype(F32)
+            for m in range(3):
+                ag_copy(m, h).start()
+
+    def wait_rs_sends():
+        for e in range(4):
+            d2d(e).wait_send()
+        for m in range(6):
+            for h in range(2):
+                rs_copy(m, h).wait_send()
+
+    def wait_ag_sends():
+        for m in range(9):
+            for h in range(2):
+                ag_copy(m, h).wait_send()
+
+    def got(m, h):
+        ag_copy(m, h).wait_recv()
+
+    def forward_first(h):
+        got(0, h)
+        got(1, h)
+        for m in (3, 4, 5, 6):
+            ag_copy(m, h).start()
+
+    def forward_second(h):
+        got(3, h)
+        ag_copy(7, h).start()
+        got(4, h)
+        ag_copy(8, h).start()
+
+    attn = attn_ref[...]
+    for t in range(8):
+        dc, e = order_cols[t]
+        wo_copy(t).wait()
+        store_block(dc, e, jnp.dot(attn, wo_buf[t % WO_SLOTS], preferred_element_type=F32))
+        if t + WO_SLOTS < 8:
+            wo_copy(t + WO_SLOTS).start()
+        elif t - WO_SLOTS < GU_SLOTS:
+            for copy in gu_copies(t - WO_SLOTS):
+                copy.start()
+        if t == 0:
+            pl.semaphore_wait(barrier, 7)
+        if dc == 1:
+            d2d(e).start()
+        elif e >= 1:
+            add_partner(e - 1)
+    for k in range(8 - WO_SLOTS, GU_SLOTS):
+        for copy in gu_copies(k):
+            copy.start()
+    for t in range(WD_SLOTS):
+        wd_copy(t).start()
+    add_partner(3)
+    resid_copy.wait()
+    reduce_scatter_rest(lambda h, ab: resid_buf[h * half:(h + 1) * half, ab * piece:(ab + 1) * piece].astype(F32))
+
+    parts = []
+    for h in range(2):
+        sq = jnp.zeros((half, 1), F32)
+        for ab in range(2):
+            vals = xg[me, h, ab]
+            sq = sq + jnp.sum(vals * vals, axis=-1, keepdims=True)
+        parts.append(sq)
+    sq = jnp.concatenate(parts, axis=0)
+    stat_out[...] = jnp.transpose(jnp.broadcast_to(sq, (rows, 128)))[:8]
+
+    def st_copy(j):
+        return remote(stat_out, stat.at[j], st_send.at[j], st_recv.at[j], (tp + j) % 8)
+
+    for j in range(1, 8):
+        st_copy(j).start()
+    sq_all = stat_out[...]
+    for j in range(1, 8):
+        st_copy(j).wait_recv()
+        sq_all = sq_all + stat[j]
+    scale = lax.rsqrt(sq_all * (1.0 / width) + EPS)
+    rbuf[...] = jnp.transpose(jnp.broadcast_to(scale[:1], (128, rows)))
+
+    def gate_up(k):
+        o = owner(*GATHER_ORDER[k])
+        for h in range(2):
+            r_half = rbuf[h * half:(h + 1) * half, :1]
+            for ab in range(2):
+                gain = gbuf[o, :, ab * piece:(ab + 1) * piece]
+                hbuf[h * half:(h + 1) * half, ab * piece:(ab + 1) * piece] = (
+                    xg[o, h, ab] * r_half * gain).astype(BF16)
+        s = k % GU_SLOTS
+        for copy in gu_copies(k):
+            copy.wait()
+        normed = hbuf[...]
+        gate = jnp.dot(normed, wg_buf[s], preferred_element_type=F32)
+        up = jnp.dot(normed, wu_buf[s], preferred_element_type=F32)
+        if k == 0:
+            acc_g[...] = gate
+            acc_u[...] = up
+        else:
+            acc_g[...] += gate
+            acc_u[...] += up
+        if k + GU_SLOTS < 8:
+            for copy in gu_copies(k + GU_SLOTS):
+                copy.start()
+
+    gate_up(0)
+    got(2, 0)
+    got(2, 1)
+    gate_up(1)
+    forward_first(0)
+    forward_first(1)
+    gate_up(2)
+    gate_up(3)
+    for h in range(2):
+        got(5, h)
+        got(6, h)
+    gate_up(4)
+    forward_second(0)
+    gate_up(5)
+    forward_second(1)
+    gate_up(6)
+    for h in range(2):
+        got(7, h)
+        got(8, h)
+    gate_up(7)
+
+    gate = acc_g[...].astype(BF16).astype(F32)
+    up = acc_u[...].astype(BF16).astype(F32)
+    abuf[...] = (jax.nn.silu(gate) * up).astype(BF16)
+
+    wait_rs_sends()
+    wait_ag_sends()
+    for t in range(8):
+        dc, e = order_cols[t]
+        wd_copy(t).wait()
+        store_block(dc, e, jnp.dot(abuf[...], wd_buf[t % WD_SLOTS], preferred_element_type=F32))
+        if t + WD_SLOTS < 8:
+            wd_copy(t + WD_SLOTS).start()
+        if dc == 1:
+            d2d(e).start()
+        elif e >= 1:
+            add_partner(e - 1)
+    add_partner(3)
+    reduce_scatter_rest(lambda h, ab: xg[me, h, ab])
+
+    def out_copy(k):
+        o = owner(*GATHER_ORDER[k])
+        return pltpu.make_async_copy(obuf.at[k], out_hbm.at[:, cols(o)], out_sem.at[k])
+
+    def write_out(k):
+        o = owner(*GATHER_ORDER[k])
+        for h in range(2):
+            for ab in range(2):
+                obuf[k, h * half:(h + 1) * half, ab * piece:(ab + 1) * piece] = xg[o, h, ab].astype(BF16)
+        out_copy(k).start()
+
+    write_out(0)
+    got(2, 0)
+    got(2, 1)
+    write_out(1)
+    forward_first(0)
+    forward_first(1)
+    write_out(2)
+    write_out(3)
+    forward_second(0)
+    for h in range(2):
+        got(5, h)
+        got(6, h)
+    write_out(4)
+    write_out(5)
+    forward_second(1)
+    write_out(6)
+    for h in range(2):
+        got(7, h)
+        got(8, h)
+    write_out(7)
+    for j in range(1, 8):
+        st_copy(j).wait_send()
+    wait_rs_sends()
+    wait_ag_sends()
+    for k in range(8):
+        out_copy(k).wait()
+
+
+def mlp_tail(attn_out, resid_in, gain_mlp, w_out, w_gate, w_up, w_down):
+    rows, width = resid_in.shape
+    depth = w_out.shape[0]
+    ffn = w_gate.shape[1]
+    block = width // 8
+    piece = block // 2
+    half = rows // 2
+    dma = pltpu.SemaphoreType.DMA
+    return pl.pallas_call(
+        tail_kernel,
+        out_shape=jax.ShapeDtypeStruct((rows, width), BF16),
+        in_specs=[pl.BlockSpec(memory_space=pltpu.VMEM)] * 2 + [pl.BlockSpec(memory_space=pl.ANY)] * 5,
+        out_specs=pl.BlockSpec(memory_space=pl.ANY),
+        scratch_shapes=[
+            pltpu.VMEM((WO_SLOTS, depth, block), BF16),
+            pltpu.VMEM((GU_SLOTS, block, ffn), BF16),
+            pltpu.VMEM((GU_SLOTS, block, ffn), BF16),
+            pltpu.VMEM((WD_SLOTS, ffn, block), BF16),
+            pltpu.VMEM((2, 4, 2, 2, half, piece), F32),
+            pltpu.VMEM((4, 2, 2, half, piece), F32),
+            pltpu.VMEM((2, 2, 2, half, piece), F32),
+            pltpu.VMEM((2, 2, half, piece), F32),
+            pltpu.VMEM((8, 2, 2, half, piece), F32),
+            pltpu.VMEM((rows, ffn), F32),
+            pltpu.VMEM((rows, ffn), F32),
+            pltpu.VMEM((rows, ffn), BF16),
+            pltpu.VMEM((rows, block), BF16),
+            pltpu.VMEM((rows, block), BF16),
+            pltpu.VMEM((8, rows, block), BF16),
+            pltpu.VMEM((8, 8, rows), F32),
+            pltpu.VMEM((8, rows), F32),
+            pltpu.VMEM((8, 1, block), F32),
+            pltpu.VMEM((rows, 128), F32),
+            dma((WO_SLOTS,)),
+            dma((2, GU_SLOTS)),
+            dma((WD_SLOTS,)),
+            dma(()),
+            dma((8,)),
+            dma((4,)),
+            dma((4,)),
+            dma((6, 2)),
+            dma((6, 2)),
+            dma((9, 2)),
+            dma((9, 2)),
+            dma((8,)),
+            dma((8,)),
+        ],
+        compiler_params=pltpu.CompilerParams(collective_id=0, has_side_effects=True,
+                                             vmem_limit_bytes=67_000_000),
+    )(attn_out, gain_mlp.reshape(1, width), resid_in, w_out, w_gate, w_up, w_down)
 
 
 def solution(mesh):
@@ -82,13 +449,7 @@
                     w_out, gain_mlp, w_gate, w_up, w_down):
         attn_out, k_full, v_full = attention_block(resid_in, positions, k_cache, v_cache,
                                                    gain_attn, w_query, w_key, w_value)
-        y_part = jnp.dot(attn_out, w_out, preferred_element_type=jnp.float32)
-        y_sum = lax.psum(y_part, 'tp')
-        resid_mid = (resid_in.astype(jnp.float32) + y_sum).astype(jnp.bfloat16)
-        hidden = gated_hidden(rms_norm(resid_mid, gain_mlp), w_gate, w_up)
-        z_part = jnp.dot(hidden, w_down, preferred_element_type=jnp.float32)
-        z_sum = lax.psum(z_part, 'tp')
-        resid_out = (resid_mid.astype(jnp.float32) + z_sum).astype(jnp.bfloat16)
+        resid_out = mlp_tail(attn_out, resid_in, gain_mlp, w_out, w_gate, w_up, w_down)
         return resid_out, k_full, v_full
 
     row_spec = P('dp', None)

time: 231 us -> 111 us (0.48)
  waiting for transfers between devices: 141 us -> 0 us
  Pallas kernels: 0 us -> 73.8 us
  matrix products: 51.8 us -> 14.8 us
  between operations: 14.2 us -> 0.79 us
  other arithmetic: 19.9 us -> 13.1 us
  local copies, waits for them, and re-layouts: 3.48 us -> 7.85 us
    psum x2 -> x0, waiting for transfers between devices: 141 us -> none  [the longest x1 71.4 us: layer_local(): y_sum = lax.psum(y_part, 'tp')]
    pallas_call x0 -> x1, Pallas kernels: none -> 73.8 us  [mlp_tail(): pl.pallas_call(tail_kernel, out_shape=jax.ShapeDtypeStruct((rows, width),...]
    dot_general x3 -> x0, matrix products: 37.5 us -> none  [the longest x1 20.6 us: layer_local(): z_part = jnp.dot(hidden, w_down, preferred_element_type=jnp.float32)]
    convert_element_type x1 -> x0, other arithmetic: 3.34 us -> none  [layer_local(): resid_out = (resid_mid.astype(jnp.float32) + z_sum).astype(jnp.bfloat16)]
    reduce_sum x2 -> x1, other arithmetic: 4.24 us -> 1.91 us  [rms_norm(): mean_sq = jnp.mean(rows_f * rows_f, axis=-1, keepdims=True)]
    unnamed x16 -> x11, local copies, waits for them, and re-layouts: 2.97 us -> 5.19 us
  transfers between devices with their start and end apart: 2 -> 0, of which waited for: 2 -> 0; matrix products, arithmetic and copies ran while one was open for 0% -> 0% of each run, Pallas kernels for 0% -> 0%
where the time goes in v1:
time: 111 us; the launch traced here: 110 us
  Pallas kernels  73.8 us (66%)
  matrix products  14.8 us (13%)
  other arithmetic  13.1 us (12%)
  local copies, waits for them, and re-layouts  7.85 us (7%)
    pallas_call x1, Pallas kernels, mlp_tail(): pl.pallas_call(tail_kernel, out_shape=jax.ShapeDtypeStruct((rows, width),...  73.8 us
    select_n x1, other arithmetic, attention_block(): k_full = jnp.where(slot_hit, key_new[:, None], k_cache)  8.49 us
    unnamed x11, local copies, waits for them, and re-layouts  5.19 us
    dot_general x1, matrix products, attention_block(): jnp.dot(normed, w_query, preferred_element_type=jnp.float32)  5.13 us
    dot_general x1, matrix products, attention_block(): jnp.einsum('bkgs,bskd->bkgd', attn_prob, v_full, preferred_element_type=j...  4.01 us
    dot_general x1, matrix products, attention_block(): jnp.dot(normed, w_value, preferred_element_type=jnp.float32)  2.53 us
    dot_general x1, matrix products, attention_block(): jnp.einsum('bkgd,bskd->bkgs', queries, k_full, preferred_element_type=jnp...  2.3 us

profile of v1, /device:TPU:0, one launch (start us, length us, event | category | flops | bytes accessed | tf_op | source)
XLA Modules:
  0.0 110.3 jit_solution(14874957055450528347)
XLA Ops:
  0.6 0.0 copy-start.1
  0.6 0.0 copy-start.2
  0.7 0.0 copy-start.3
  0.7 0.8 convert_element_type.57
  1.5 1.9 %fusion.5 = f32[128]{0:T(128)S(1)} fusion(bf16[128,6144]{1,0:T(8,128)(2,1)} %resid_hbm.1), kind=kLoop, calls=%fused_computation.9 | loop fusion | flops 2359168 | bytes 1573376 | tf_op jit(solution)/shard_map/reduce_sum | solution.py:19
  3.4 0.7 convert_element_type.52
  4.1 1.3 %reshape.246.gain_ref = bf16[1,6144]{1,0:T(2,128)(2,1)} reshape(bf16[6144]{0:T(1024)(128)(2,1)} %param.22) | data formatting | bytes 24576 | tf_op jit(solution)/shard_map/reshape | solution.py:444
  5.5 2.5 %convolution_convert_fusion.1 = bf16[128,128]{1,0:T(8,128)(2,1)S(1)} fusion(bf16[6144,128]{1,0:T(8,128)(2,1)} %param.20, bf16[128,6144]{1,0:T(8,128)(2,1)} %resid_hbm.1, f32[6144]{0:T(1024)S(1)} %convert_element_type.52, f32[128]{0:T(128)S(1)} %add_rsqrt_fusion), kind=kOutput, calls=%fused_computation.19 | convolution fusion | flops 204488704 | bytes 3203584 | tf_op jit(solution)/shard_map/dot_general | solution.py:55
  8.0 0.0 copy-done.2
  8.0 0.1 iota_compare_fusion.1
  8.1 0.0 copy-done.1
  8.1 0.0 copy-done.3
  8.1 0.9 fusion.21
  9.0 0.2 fusion.35
  9.2 0.1 copy.20
  9.3 0.3 multiply_cosine_fusion
  9.7 5.1 %fusion.19 = f32[128,768]{1,0:T(8,128)S(1)} fusion(bf16[6144,768]{1,0:T(8,128)(2,1)} %param.18, bf16[128,6144]{1,0:T(8,128)(2,1)S(1)} %copy-done.1, f32[6144]{0:T(1024)S(1)} %convert_element_type.52, f32[128]{0:T(128)S(1)} %add_rsqrt_fusion), kind=kOutput, calls=%fused_computation.18 | convolution fusion | flops 1211301888 | bytes 11428352 | tf_op jit(solution)/shard_map/dot_general | solution.py:53
  14.8 0.2 copy.17
  15.0 0.2 copy.24
  15.2 0.2 copy.23
  15.5 0.1 subtract_convert_fusion
  15.6 8.5 %broadcast_select_fusion.1 = (bf16[128,128,1,128]{3,1,2,0:T(8,128)(2,1)S(1)}, bf16[128,128,1,128]{3,1,2,0:T(8,128)(2,1)}) fusion(bf16[128,128,1,128]{3,1,2,0:T(8,128)(2,1)} %param.15, pred[128,128]{1,0:T(8,128)(4,1)S(1)} %get-tuple-element.14, bf16[128,128]{1,0:T(8,128)(2,1)S(1)} %copy.20, bf16[128,128,1,128]{3,1,2,0:T(8,128)(2,1)} %param.16, ...), kind=kLoop, calls=%fused_computation.6 | loop fusion | flops 4194304 | bytes 16859136 | tf_op jit(solution)/shard_map/jit(_where)/select_n | solution.py:64
  24.1 0.0 copy-start
  24.1 2.0 %copy-done = bf16[128,128,1,128]{3,1,2,0:T(8,128)(2,1)} copy-done((bf16[128,128,1,128]{3,1,2,0:T(8,128)(2,1)}, bf16[128,128,1,128]{3,1,2,0:T(8,128)(2,1)S(1)}, u32[]{:S(2)}) %copy-start) | copy-done | bytes 4194328
  26.1 2.3 %fusion.13 = f32[128,6,128]{2,1,0:T(8,128)S(1)} fusion(bf16[128,128,1,128]{3,1,2,0:T(8,128)(2,1)S(1)} %get-tuple-element.19, bf16[128,6,64]{2,1,0:T(8,128)(2,1)S(1)} %get-tuple-element.4, bf16[128,6,64]{2,1,0:T(8,128)(2,1)S(1)} %get-tuple-element.3, pred[128,128]{1,0:T(8,128)(4,1)S(1)} %get-tuple-element.13), kind=kOutput, calls=%fused_computation.15 | convolution fusion | flops 25755648 | bytes 4800512 | tf_op jit(solution)/shard_map/bkgd,bskd->bkgs/dot_general | solution.py:66
  28.4 0.4 fusion.41
  28.8 4.0 %fusion.16 = bf16[128,6,128]{2,1,0:T(8,128)(2,1)S(1)} fusion(bf16[128,128,1,128]{3,1,2,0:T(8,128)(2,1)} %get-tuple-element.20, f32[128,6]{1,0:T(8,128)S(1)} %fusion.41, f32[128,6,128]{2,1,0:T(8,128)S(1)} %fusion.13), kind=kOutput, calls=%fused_computation.16 | convolution fusion | flops 25559936 | bytes 4787200 | tf_op jit(solution)/shard_map/bkgs,bskd->bkgd/dot_general | solution.py:71
  32.8 0.2 copy.21
  33.0 0.8 copy.22.attn_ref
  33.9 73.8 %shard_map.148 = bf16[128,6144]{1,0:T(8,128)(2,1)} custom-call(bf16[128,768]{1,0:T(8,128)(2,1)} %copy.22.attn_ref, bf16[1,6144]{1,0:T(2,128)(2,1)} %reshape.246.gain_ref, bf16[128,6144]{1,0:T(8,128)(2,1)} %resid_hbm.1, bf16[768,6144]{1,0:T(8,128)(2,1)} %wo_hbm.1, bf16[6144,2048]{1,0:T(8,128)(2,1)} %wg_hbm.1, bf16[6144,2048]{1,0:T(8,128)(2,1)} %wu_hbm.1, ...), custom_call_target="tpu_custom_call" | custom-call | tf_op jit(solution)/shard_map/pallas_call | solution.py:403
  107.6 2.7 %copy.26 = bf16[128,6144]{1,0:T(8,128)(2,1)} copy(bf16[128,6144]{1,0:T(8,128)(2,1)} %shard_map.148) | data formatting | bytes 3145728
  (4 shorter events, 0.1 us)
Async XLA Ops:
  0.6 7.5 %copy-start.1 = (bf16[128,6144]{1,0:T(8,128)(2,1)S(1)}, bf16[128,6144]{1,0:T(8,128)(2,1)}, u32[]{:S(2)}) copy-start(bf16[128,6144]{1,0:T(8,128)(2,1)} %resid_hbm.1) | copy-start | bytes 4718596
  0.6 7.3 %copy-start.2 = (s32[128]{0:T(128)S(1)}, s32[128]{0:T(128)}, u32[]{:S(2)}) copy-start(s32[128]{0:T(128)} %param.14) | copy-start | bytes 1540
  0.7 7.4 %copy-start.3 = (bf16[6144,128]{1,0:T(8,128)(2,1)S(1)}, bf16[6144,128]{1,0:T(8,128)(2,1)}, u32[]{:S(2)}) copy-start(bf16[6144,128]{1,0:T(8,128)(2,1)} %param.19) | copy-start | bytes 4718596
  24.1 2.0 %copy-start = (bf16[128,128,1,128]{3,1,2,0:T(8,128)(2,1)}, bf16[128,128,1,128]{3,1,2,0:T(8,128)(2,1)S(1)}, u32[]{:S(2)}) copy-start(bf16[128,128,1,128]{3,1,2,0:T(8,128)(2,1)S(1)} %get-tuple-element.19) | copy-start | bytes 12582916

commit v2 on v1

--- a/solution.py
+++ b/solution.py
@@ -14,13 +14,13 @@
 ORIG_CTX = 8192.0
 
 
-def rms_norm(rows_in, gain):
-    rows_f = rows_in.astype(jnp.float32)
-    mean_sq = jnp.mean(rows_f * rows_f, axis=-1, keepdims=True)
-    return (rows_f * lax.rsqrt(mean_sq + EPS) * gain.astype(jnp.float32)).astype(jnp.bfloat16)
-
-
-def rope_tables(positions, head_dim):
+F32 = jnp.float32
+BF16 = jnp.bfloat16
+BLOCK_SEQS = 32
+N_CHUNKS = 6
+
+
+def inverse_frequencies(head_dim):
     half_dim = head_dim // 2
     exponents = jnp.arange(half_dim, dtype=jnp.float32) * (2.0 / head_dim)
     inv_freq = 1.0 / jnp.power(ROPE_THETA, exponents)
@@ -29,52 +29,175 @@
     blended = (1.0 - smooth) * inv_freq / ROPE_FACTOR + smooth * inv_freq
     inv_freq = jnp.where(wavelen < ORIG_CTX / HIGH_FACTOR, inv_freq,
                          jnp.where(wavelen > ORIG_CTX / LOW_FACTOR, inv_freq / ROPE_FACTOR, blended))
-    angles = positions.astype(jnp.float32)[:, None] * inv_freq[None, :]
-    return jnp.cos(angles), jnp.sin(angles)
-
-
-def apply_rope(vectors, cos_t, sin_t):
-    half_dim = vectors.shape[-1] // 2
-    lower_half = vectors[..., :half_dim]
-    upper_half = vectors[..., half_dim:]
-    cos_b = cos_t[:, None, :]
-    sin_b = sin_t[:, None, :]
-    return jnp.concatenate([lower_half * cos_b - upper_half * sin_b,
-                            upper_half * cos_b + lower_half * sin_b], axis=-1)
-
-
-def attention_block(resid_in, positions, k_cache, v_cache, gain_attn, w_query, w_key, w_value):
-    n_seqs = resid_in.shape[0]
-    cache_len = k_cache.shape[1]
-    kv_heads = k_cache.shape[2]
-    head_dim = k_cache.shape[3]
-    group_size = w_query.shape[1] // (kv_heads * head_dim)
-    normed = rms_norm(resid_in, gain_attn)
-    queries = jnp.dot(normed, w_query, preferred_element_type=jnp.float32).astype(jnp.bfloat16)
-    key_new = jnp.dot(normed, w_key, preferred_element_type=jnp.float32).astype(jnp.bfloat16)
-    value_new = jnp.dot(normed, w_value, preferred_element_type=jnp.float32).astype(jnp.bfloat16)
-    cos_t, sin_t = rope_tables(positions, head_dim)
-    queries = apply_rope(queries.reshape(n_seqs, kv_heads * group_size, head_dim).astype(jnp.float32), cos_t, sin_t)
-    queries = queries.astype(jnp.bfloat16).reshape(n_seqs, kv_heads, group_size, head_dim)
-    key_new = apply_rope(key_new.reshape(n_seqs, kv_heads, head_dim).astype(jnp.float32), cos_t, sin_t)
-    key_new = key_new.astype(jnp.bfloat16)
-    value_new = value_new.reshape(n_seqs, kv_heads, head_dim)
-    slot_iota = lax.broadcasted_iota(jnp.int32, (n_seqs, cache_len), 1)
-    slot_hit = (slot_iota == positions[:, None])[:, :, None, None]
-    k_full = jnp.where(slot_hit, key_new[:, None], k_cache)
-    v_full = jnp.where(slot_hit, value_new[:, None], v_cache)
-    scores = jnp.einsum('bkgd,bskd->bkgs', queries, k_full, preferred_element_type=jnp.float32)
-    scores = scores * (1.0 / math.sqrt(head_dim))
-    valid = (slot_iota <= positions[:, None])[:, None, None, :]
-    scores = jnp.where(valid, scores, -jnp.inf)
-    attn_prob = jax.nn.softmax(scores, axis=-1).astype(jnp.bfloat16)
-    attn_out = jnp.einsum('bkgs,bskd->bkgd', attn_prob, v_full, preferred_element_type=jnp.float32)
-    attn_out = attn_out.astype(jnp.bfloat16).reshape(n_seqs, kv_heads * group_size * head_dim)
-    return attn_out, k_full, v_full
-
-
-F32 = jnp.float32
-BF16 = jnp.bfloat16
+    return jnp.concatenate([inv_freq, inv_freq]).reshape(1, head_dim)
+
+
+def attention_kernel(pos_ref, pos_row_ref, inv_ref, gain_ref, resid_hbm, wq_hbm, wk_hbm, wv_hbm, kc_hbm, vc_hbm,
+                     out_ref, ko_hbm, vo_hbm,
+                     resid_buf, hbuf, gbuf, wbuf, kbuf, vbuf, acc, qbuf, knew, vnew, obuf,
+                     resid_sem, w_sem, in_sem, back_sem):
+    rows, width = hbuf.shape
+    q_width = wq_hbm.shape[1]
+    head_dim = kbuf.shape[2]
+    slots = kbuf.shape[1]
+    heads = q_width // head_dim
+    chunk = width // N_CHUNKS
+    tiles = width // 128
+    n_blocks = rows // BLOCK_SEQS
+
+    resid_copy = pltpu.make_async_copy(resid_hbm, resid_buf, resid_sem)
+    resid_copy.start()
+
+    def w_copies(i):
+        r = pl.ds(i * chunk, chunk)
+        return (pltpu.make_async_copy(wq_hbm.at[r], wbuf.at[i, :, pl.ds(0, q_width)], w_sem.at[i, 0]),
+                pltpu.make_async_copy(wk_hbm.at[r], wbuf.at[i, :, pl.ds(q_width, head_dim)], w_sem.at[i, 1]),
+                pltpu.make_async_copy(wv_hbm.at[r], wbuf.at[i, :, pl.ds(q_width + head_dim, head_dim)],
+                                      w_sem.at[i, 2]))
+
+    def cache_in(blk):
+        r = pl.ds(blk * BLOCK_SEQS, BLOCK_SEQS)
+        return (pltpu.make_async_copy(kc_hbm.at[r], kbuf.at[r], in_sem.at[0, blk]),
+                pltpu.make_async_copy(vc_hbm.at[r], vbuf.at[r], in_sem.at[1, blk]))
+
+    def cache_back(blk):
+        r = pl.ds(blk * BLOCK_SEQS, BLOCK_SEQS)
+        return (pltpu.make_async_copy(kbuf.at[r], ko_hbm.at[r], back_sem.at[0, blk]),
+                pltpu.make_async_copy(vbuf.at[r], vo_hbm.at[r], back_sem.at[1, blk]))
+
+    for i in range(N_CHUNKS):
+        for copy in w_copies(i):
+            copy.start()
+
+    pos_rows = jnp.transpose(jnp.broadcast_to(pos_row_ref[...].astype(F32), (head_dim, rows)))
+    angles = pos_rows * inv_ref[...]
+    cos_t = jnp.cos(angles)
+    sin_t = jnp.sin(angles)
+    lanes = lax.broadcasted_iota(jnp.int32, (rows, head_dim), 1)
+    sin_t = jnp.where(lanes < head_dim // 2, -sin_t, sin_t)
+
+    def rope(v):
+        v = v.astype(BF16).astype(F32)
+        return (v * cos_t + pltpu.roll(v, head_dim // 2, 1) * sin_t).astype(BF16).astype(F32)
+
+    gbuf[...] = gain_ref[...].astype(F32)
+    qbuf[...] = jnp.zeros_like(qbuf)
+
+    resid_copy.wait()
+    sq = jnp.zeros((rows, 128), F32)
+    for j in range(tiles):
+        vals = resid_buf[:, j * 128:(j + 1) * 128].astype(F32)
+        sq = sq + vals * vals
+    scale = lax.rsqrt(jnp.sum(sq, axis=-1, keepdims=True) * (1.0 / width) + EPS)
+    scale = jnp.broadcast_to(scale, (rows, 128))
+    for j in range(tiles):
+        vals = resid_buf[:, j * 128:(j + 1) * 128].astype(F32)
+        hbuf[:, j * 128:(j + 1) * 128] = (vals * scale * gbuf[j:j + 1, :]).astype(BF16)
+
+    for i in range(N_CHUNKS):
+        for copy in w_copies(i):
+            copy.wait()
+        if 1 <= i <= n_blocks:
+            for copy in cache_in(i - 1):
+                copy.start()
+        part = jnp.dot(hbuf[:, i * chunk:(i + 1) * chunk], wbuf[i], preferred_element_type=F32)
+        if i == 0:
+            acc[...] = part
+        else:
+            acc[...] += part
+    for h in range(heads):
+        qbuf[:, h, :] = rope(acc[:, h * head_dim:(h + 1) * head_dim])
+    knew[...] = rope(acc[:, q_width:q_width + head_dim])
+    vnew[...] = acc[:, q_width + head_dim:q_width + 2 * head_dim].astype(BF16).astype(F32)
+
+    sub_iota = lax.broadcasted_iota(jnp.int32, (16, head_dim), 0)
+    lane_iota = lax.broadcasted_iota(jnp.int32, (8, slots), 1)
+    inv_sqrt = 1.0 / math.sqrt(head_dim)
+
+    def block_step(blk, carry):
+        first = blk * BLOCK_SEQS
+        for copy in cache_in(blk):
+            copy.wait()
+        pos = [pos_ref[first + j] for j in range(BLOCK_SEQS)]
+        for buf, new in ((kbuf, knew), (vbuf, vnew)):
+            for j0 in range(0, BLOCK_SEQS, 16):
+                merged = []
+                for j in range(j0, j0 + 16):
+                    base = pl.multiple_of((pos[j] // 16) * 16, 16)
+                    old = buf[first + j, pl.ds(base, 16), :].astype(F32)
+                    row = jnp.broadcast_to(new[pl.ds(first + j, 1), :], (16, head_dim))
+                    merged.append((base, jnp.where(sub_iota == pos[j] - base, row, old).astype(BF16)))
+                for j in range(j0, j0 + 16):
+                    base, tile = merged[j - j0]
+                    buf[first + j, pl.ds(base, 16), :] = tile
+        probs = []
+        for j in range(0, BLOCK_SEQS, 2):
+            q2 = qbuf[pl.ds(first + j, 2)].reshape(16, head_dim).astype(BF16)
+            k2 = kbuf[pl.ds(first + j, 2)].reshape(2 * slots, head_dim)
+            scores = lax.dot_general(q2, k2, (((1,), (1,)), ((), ())), preferred_element_type=F32)
+            pair = []
+            for i in range(2):
+                s_one = scores[8 * i:8 * (i + 1), slots * i:slots * (i + 1)] * inv_sqrt
+                s_one = jnp.where(lane_iota <= pos[j + i], s_one, -jnp.inf)
+                s_one = jnp.exp(s_one - jnp.max(s_one, axis=-1, keepdims=True))
+                pair.append(s_one / jnp.sum(s_one, axis=-1, keepdims=True))
+            probs.append(jnp.concatenate(pair, axis=0).astype(BF16))
+        for j in range(0, BLOCK_SEQS, 2):
+            v2 = jnp.concatenate([vbuf[first + j], vbuf[first + j + 1]], axis=1)
+            both = jnp.dot(probs[j // 2], v2, preferred_element_type=F32)
+            for i in range(2):
+                obuf[first + j + i] = both[8 * i:8 * (i + 1), head_dim * i:head_dim * (i + 1)]
+        for copy in cache_back(blk):
+            copy.start()
+        return carry
+
+    lax.fori_loop(0, n_blocks, block_step, 0)
+    for h in range(heads):
+        out_ref[:, h * head_dim:(h + 1) * head_dim] = obuf[:, h, :].astype(BF16)
+    for blk in range(n_blocks):
+        for copy in cache_back(blk):
+            copy.wait()
+
+
+def attention(resid_in, positions, k_cache, v_cache, gain_attn, w_query, w_key, w_value):
+    rows, width = resid_in.shape
+    slots, head_dim = k_cache.shape[1], k_cache.shape[3]
+    q_width = w_query.shape[1]
+    qkv = q_width + 2 * head_dim
+    n_blocks = rows // BLOCK_SEQS
+    dma = pltpu.SemaphoreType.DMA
+    flat = (rows, slots, head_dim)
+    vmem = pl.BlockSpec(memory_space=pltpu.VMEM)
+    anywhere = pl.BlockSpec(memory_space=pl.ANY)
+    attn_out, k_full, v_full = pl.pallas_call(
+        attention_kernel,
+        out_shape=(jax.ShapeDtypeStruct((rows, q_width), BF16),
+                   jax.ShapeDtypeStruct(flat, BF16), jax.ShapeDtypeStruct(flat, BF16)),
+        in_specs=[pl.BlockSpec(memory_space=pltpu.SMEM), vmem, vmem, vmem] + [anywhere] * 6,
+        out_specs=(vmem, anywhere, anywhere),
+        scratch_shapes=[
+            pltpu.VMEM((rows, width), BF16),
+            pltpu.VMEM((rows, width), BF16),
+            pltpu.VMEM((width // 128, 128), F32),
+            pltpu.VMEM((N_CHUNKS, width // N_CHUNKS, qkv), BF16),
+            pltpu.VMEM(flat, BF16),
+            pltpu.VMEM(flat, BF16),
+            pltpu.VMEM((rows, qkv), F32),
+            pltpu.VMEM((rows, 8, head_dim), F32),
+            pltpu.VMEM((rows, head_dim), F32),
+            pltpu.VMEM((rows, head_dim), F32),
+            pltpu.VMEM((rows, 8, head_dim), F32),
+            dma(()),
+            dma((N_CHUNKS, 3)),
+            dma((2, n_blocks)),
+            dma((2, n_blocks)),
+        ],
+        compiler_params=pltpu.CompilerParams(vmem_limit_bytes=60_000_000),
+    )(positions, positions.reshape(1, rows), inverse_frequencies(head_dim), gain_attn.reshape(width // 128, 128),
+      resid_in, w_query, w_key, w_value, k_cache.reshape(flat), v_cache.reshape(flat))
+    return attn_out, k_full.reshape(k_cache.shape), v_full.reshape(v_cache.shape)
+
+
 REL = ((1, 1), (0, 1), (1, 0), (0, 0))
 WO_SLOTS = 4
 GU_SLOTS = 5
@@ -146,8 +269,7 @@
     for j in range(1, 8):
         pl.semaphore_signal(barrier, inc=1, device_id={'tp': (tp + j) % 8}, device_id_type=pl.DeviceIdType.MESH)
 
-    for o in range(8):
-        gbuf[o] = gain_ref[:, o * block:(o + 1) * block].astype(F32)
+    gbuf[...] = gain_ref[...].astype(F32)
 
     def store_block(dc, e, res):
         for h in range(2):
@@ -292,11 +414,12 @@
     def gate_up(k):
         o = owner(*GATHER_ORDER[k])
         for h in range(2):
-            r_half = rbuf[h * half:(h + 1) * half, :1]
+            r_half = rbuf[h * half:(h + 1) * half, :]
             for ab in range(2):
-                gain = gbuf[o, :, ab * piece:(ab + 1) * piece]
-                hbuf[h * half:(h + 1) * half, ab * piece:(ab + 1) * piece] = (
-                    xg[o, h, ab] * r_half * gain).astype(BF16)
+                for j in range(piece // 128):
+                    gain = gbuf[pl.ds(o * (block // 128) + ab * (piece // 128) + j, 1), :]
+                    hbuf[h * half:(h + 1) * half, ab * piece + j * 128:ab * piece + (j + 1) * 128] = (
+                        xg[o, h, ab, :, j * 128:(j + 1) * 128] * r_half * gain).astype(BF16)
         s = k % GU_SLOTS
         for copy in gu_copies(k):
             copy.wait()
@@ -423,7 +546,7 @@
             pltpu.VMEM((8, rows, block), BF16),
             pltpu.VMEM((8, 8, rows), F32),
             pltpu.VMEM((8, rows), F32),
-            pltpu.VMEM((8, 1, block), F32),
+            pltpu.VMEM((width // 128, 128), F32),
             pltpu.VMEM((rows, 128), F32),
             dma((WO_SLOTS,)),
             dma((2, GU_SLOTS)),
@@ -441,14 +564,14 @@
         ],
         compiler_params=pltpu.CompilerParams(collective_id=0, has_side_effects=True,
                                              vmem_limit_bytes=67_000_000),
-    )(attn_out, gain_mlp.reshape(1, width), resid_in, w_out, w_gate, w_up, w_down)
+    )(attn_out, gain_mlp.reshape(width // 128, 128), resid_in, w_out, w_gate, w_up, w_down)
 
 
 def solution(mesh):
     def layer_local(resid_in, positions, k_cache, v_cache, gain_attn, w_query, w_key, w_value,
                     w_out, gain_mlp, w_gate, w_up, w_down):
-        attn_out, k_full, v_full = attention_block(resid_in, positions, k_cache, v_cache,
-                                                   gain_attn, w_query, w_key, w_value)
+        attn_out, k_full, v_full = attention(resid_in, positions, k_cache, v_cache, gain_attn,
+                                             w_query, w_key, w_value)
         resid_out = mlp_tail(attn_out, resid_in, gain_mlp, w_out, w_gate, w_up, w_down)
         return resid_out, k_full, v_full
 

time: 111 us -> 92.9 us (0.84)
  matrix products: 14.8 us -> 0 us
  Pallas kernels: 73.8 us -> 88.2 us
  other arithmetic: 13.1 us -> 0.6 us
  local copies, waits for them, and re-layouts: 7.85 us -> 2.69 us
    dot_general x5 -> x0, matrix products: 14.8 us -> none  [the longest x1 5.13 us: attention_block(): jnp.dot(normed, w_query, preferred_element_type=jnp.float32)]
    pallas_call x0 -> x1, Pallas kernels: none -> 14.6 us  [attention(): pl.pallas_call(attention_kernel, out_shape=(jax.ShapeDtypeStruct((rows, q...]
    select_n x2 -> x1, other arithmetic: 8.51 us -> 0.02 us  [inverse_frequencies(): jnp.where(wavelen < ORIG_CTX / HIGH_FACTOR, inv_freq, jnp.where(wavelen >...]
    unnamed x11 -> x1, local copies, waits for them, and re-layouts: 5.19 us -> 2.69 us
    reshape x2 -> x0, local copies, waits for them, and re-layouts: 2.15 us -> none  [the longest x1 1.32 us: mlp_tail(): gain_mlp.reshape(1, width)]
    reduce_sum x1 -> x0, other arithmetic: 1.91 us -> none  [rms_norm(): mean_sq = jnp.mean(rows_f * rows_f, axis=-1, keepdims=True)]
    convert_element_type x2 -> x0, other arithmetic: 1.53 us -> none  [the longest x1 0.81 us: rope_tables(): angles = positions.astype(jnp.float32)[:, None] * inv_freq[None, :]]
where the time goes in v2:
time: 92.9 us; the launch traced here: 92.1 us
  Pallas kernels  88.2 us (95%)
  local copies, waits for them, and re-layouts  2.69 us (3%)
    pallas_call x1, Pallas kernels, mlp_tail(): pl.pallas_call(tail_kernel, out_shape=jax.ShapeDtypeStruct((rows, width),...  73.5 us
    pallas_call x1, Pallas kernels, attention(): pl.pallas_call(attention_kernel, out_shape=(jax.ShapeDtypeStruct((rows, q...  14.6 us
    unnamed x1, local copies, waits for them, and re-layouts  2.69 us

profile of v2, /device:TPU:0, one launch (start us, length us, event | category | flops | bytes accessed | tf_op | source)
XLA Modules:
  0.0 92.1 jit_solution(10048708677462360990)
XLA Ops:
  0.7 0.6 maximum_bitcast_fusion.inv_ref
  1.2 14.6 %shard_map.148 = (bf16[128,768]{1,0:T(8,128)(2,1)}, bf16[128,128,128]{2,1,0:T(8,128)(2,1)}, bf16[128,128,128]{2,1,0:T(8,128)(2,1)}) custom-call(s32[128]{0:T(128)} %pos_ref.1, s32[1,128]{1,0:T(1,128)} %bitcast.17, f32[1,128]{1,0:T(1,128)} %maximum_bitcast_fusion.inv_ref, bf16[48,128]{1,0:T(8,128)(2,1)} %bitcast.15, bf16[128,6144]{1,0:T(8,128)(2,1)} %resid_hbm.3, ...), custom_call_target="tpu_custom_call" | custom-call | tf_op jit(solution)/shard_map/pallas_call | solution.py:172
  15.9 73.5 %shard_map.149 = bf16[128,6144]{1,0:T(8,128)(2,1)} custom-call(bf16[128,768]{1,0:T(8,128)(2,1)} %get-tuple-element.6.attn_ref, bf16[48,128]{1,0:T(8,128)(2,1)} %bitcast.16, bf16[128,6144]{1,0:T(8,128)(2,1)} %resid_hbm.3, bf16[768,6144]{1,0:T(8,128)(2,1)} %wo_hbm.1, bf16[6144,2048]{1,0:T(8,128)(2,1)} %wg_hbm.1, bf16[6144,2048]{1,0:T(8,128)(2,1)} %wu_hbm.1, ...), custom_call_target="tpu_custom_call" | custom-call | tf_op jit(solution)/shard_map/pallas_call | solution.py:526
  89.4 2.7 %copy.19 = bf16[128,6144]{1,0:T(8,128)(2,1)} copy(bf16[128,6144]{1,0:T(8,128)(2,1)} %shard_map.149) | data formatting | bytes 3145728
  (1 shorter events, 0.0 us)

commit v3 on v2

--- a/solution.py
+++ b/solution.py
@@ -1,5 +1,6 @@
 import math
 import jax
+import numpy as np
 import jax.numpy as jnp
 from jax import lax
 from jax.experimental import pallas as pl
@@ -20,22 +21,30 @@
 N_CHUNKS = 6
 
 
+def in_hbm(x):
+    return pltpu.with_memory_space_constraint(x, pltpu.HBM)
+
+
+def in_vmem(x):
+    return pltpu.with_memory_space_constraint(x, pltpu.VMEM)
+
+
 def inverse_frequencies(head_dim):
-    half_dim = head_dim // 2
-    exponents = jnp.arange(half_dim, dtype=jnp.float32) * (2.0 / head_dim)
-    inv_freq = 1.0 / jnp.power(ROPE_THETA, exponents)
-    wavelen = (2.0 * math.pi) / inv_freq
-    smooth = (ORIG_CTX / wavelen - LOW_FACTOR) / (HIGH_FACTOR - LOW_FACTOR)
-    blended = (1.0 - smooth) * inv_freq / ROPE_FACTOR + smooth * inv_freq
-    inv_freq = jnp.where(wavelen < ORIG_CTX / HIGH_FACTOR, inv_freq,
-                         jnp.where(wavelen > ORIG_CTX / LOW_FACTOR, inv_freq / ROPE_FACTOR, blended))
-    return jnp.concatenate([inv_freq, inv_freq]).reshape(1, head_dim)
-
-
-def attention_kernel(pos_ref, pos_row_ref, inv_ref, gain_ref, resid_hbm, wq_hbm, wk_hbm, wv_hbm, kc_hbm, vc_hbm,
+    exponents = np.arange(head_dim // 2, dtype=np.float32) * np.float32(2.0 / head_dim)
+    inv_freq = (np.float32(1.0) / np.power(np.float32(ROPE_THETA), exponents)).astype(np.float32)
+    wavelen = np.float32(2.0 * math.pi) / inv_freq
+    smooth = (np.float32(ORIG_CTX) / wavelen - np.float32(LOW_FACTOR)) / np.float32(HIGH_FACTOR - LOW_FACTOR)
+    blended = (np.float32(1.0) - smooth) * inv_freq / np.float32(ROPE_FACTOR) + smooth * inv_freq
+    inv_freq = np.where(wavelen < ORIG_CTX / HIGH_FACTOR, inv_freq,
+                        np.where(wavelen > ORIG_CTX / LOW_FACTOR, inv_freq / np.float32(ROPE_FACTOR), blended))
+    return jnp.asarray(np.concatenate([inv_freq, inv_freq]).astype(np.float32).reshape(1, head_dim))
+
+
+def attention_kernel(pos_hbm, pos_row_hbm, inv_hbm, gain_hbm, resid_hbm, wq_hbm, wk_hbm, wv_hbm, kc_hbm, vc_hbm,
                      out_ref, ko_hbm, vo_hbm,
+                     pos_ref, pos_row_ref, inv_ref, gain_ref,
                      resid_buf, hbuf, gbuf, wbuf, kbuf, vbuf, acc, qbuf, knew, vnew, obuf,
-                     resid_sem, w_sem, in_sem, back_sem):
+                     small_sem, resid_sem, w_sem, in_sem, back_sem):
     rows, width = hbuf.shape
     q_width = wq_hbm.shape[1]
     head_dim = kbuf.shape[2]
@@ -47,6 +56,10 @@
 
     resid_copy = pltpu.make_async_copy(resid_hbm, resid_buf, resid_sem)
     resid_copy.start()
+    small_copies = [pltpu.make_async_copy(src, dst, small_sem.at[i]) for i, (src, dst) in enumerate((
+        (pos_row_hbm, pos_row_ref), (inv_hbm, inv_ref), (gain_hbm, gain_ref), (pos_hbm, pos_ref)))]
+    for copy in small_copies:
+        copy.start()
 
     def w_copies(i):
         r = pl.ds(i * chunk, chunk)
@@ -69,6 +82,8 @@
         for copy in w_copies(i):
             copy.start()
 
+    for copy in small_copies:
+        copy.wait()
     pos_rows = jnp.transpose(jnp.broadcast_to(pos_row_ref[...].astype(F32), (head_dim, rows)))
     angles = pos_rows * inv_ref[...]
     cos_t = jnp.cos(angles)
@@ -171,11 +186,15 @@
     anywhere = pl.BlockSpec(memory_space=pl.ANY)
     attn_out, k_full, v_full = pl.pallas_call(
         attention_kernel,
-        out_shape=(jax.ShapeDtypeStruct((rows, q_width), BF16),
+        out_shape=(pltpu.VMEM((rows, q_width), BF16),
                    jax.ShapeDtypeStruct(flat, BF16), jax.ShapeDtypeStruct(flat, BF16)),
-        in_specs=[pl.BlockSpec(memory_space=pltpu.SMEM), vmem, vmem, vmem] + [anywhere] * 6,
+        in_specs=[anywhere] * 10,
         out_specs=(vmem, anywhere, anywhere),
         scratch_shapes=[
+            pltpu.SMEM((rows,), jnp.int32),
+            pltpu.VMEM((1, rows), jnp.int32),
+            pltpu.VMEM((1, head_dim), F32),
+            pltpu.VMEM((width // 128, 128), BF16),
             pltpu.VMEM((rows, width), BF16),
             pltpu.VMEM((rows, width), BF16),
             pltpu.VMEM((width // 128, 128), F32),
@@ -187,14 +206,16 @@
             pltpu.VMEM((rows, head_dim), F32),
             pltpu.VMEM((rows, head_dim), F32),
             pltpu.VMEM((rows, 8, head_dim), F32),
+            dma((4,)),
             dma(()),
             dma((N_CHUNKS, 3)),
             dma((2, n_blocks)),
             dma((2, n_blocks)),
         ],
-        compiler_params=pltpu.CompilerParams(vmem_limit_bytes=60_000_000),
-    )(positions, positions.reshape(1, rows), inverse_frequencies(head_dim), gain_attn.reshape(width // 128, 128),
-      resid_in, w_query, w_key, w_value, k_cache.reshape(flat), v_cache.reshape(flat))
+        compiler_params=pltpu.CompilerParams(vmem_limit_bytes=64_000_000),
+    )(*map(in_hbm, (positions, positions.reshape(1, rows), inverse_frequencies(head_dim),
+                    gain_attn.reshape(width // 128, 128), resid_in, w_query, w_key, w_value,
+                    k_cache.reshape(flat), v_cache.reshape(flat))))
     return attn_out, k_full.reshape(k_cache.shape), v_full.reshape(v_cache.shape)
 
 
@@ -209,10 +230,10 @@
     return 1 - coord if do_flip else coord
 
 
-def tail_kernel(attn_ref, gain_ref, resid_hbm, wo_hbm, wg_hbm, wu_hbm, wd_hbm, out_hbm,
+def tail_kernel(attn_ref, gain_hbm, resid_hbm, wo_hbm, wg_hbm, wu_hbm, wd_hbm, out_ref,
                 wo_buf, wg_buf, wu_buf, wd_buf, ybuf, dbuf, r1, r2, xg, acc_g, acc_u, abuf, hbuf,
-                resid_buf, obuf, stat, stat_out, gbuf, rbuf,
-                wo_sem, gu_sem, wd_sem, resid_sem, out_sem, d_send, d_recv, rs_send, rs_recv,
+                resid_buf, stat, stat_out, gain_buf, gbuf, rbuf,
+                wo_sem, gu_sem, wd_sem, resid_sem, gain_sem, d_send, d_recv, rs_send, rs_recv,
                 ag_send, ag_recv, st_send, st_recv):
     rows = attn_ref.shape[0]
     half = rows // 2
@@ -264,12 +285,12 @@
         wo_copy(t).start()
     resid_copy = pltpu.make_async_copy(resid_hbm.at[:, cols(me)], resid_buf, resid_sem)
     resid_copy.start()
+    gain_copy = pltpu.make_async_copy(gain_hbm, gain_buf, gain_sem)
+    gain_copy.start()
 
     barrier = pltpu.get_barrier_semaphore()
     for j in range(1, 8):
         pl.semaphore_signal(barrier, inc=1, device_id={'tp': (tp + j) % 8}, device_id_type=pl.DeviceIdType.MESH)
-
-    gbuf[...] = gain_ref[...].astype(F32)
 
     def store_block(dc, e, res):
         for h in range(2):
@@ -318,7 +339,7 @@
         )[m]
         return remote(ref, ref, ag_send.at[m, h], ag_recv.at[m, h], dev)
 
-    def reduce_scatter_rest(first_half_terms):
+    def reduce_scatter_rest(residual, before_last=None):
         for h in range(2):
             rs_copy(3, h).wait_recv()
             ybuf[0, 1, h, 1] = ybuf[0, 1, h, 1] + r1[1, 0, h]
@@ -333,7 +354,9 @@
             rs_copy(5, h).wait_recv()
             for ab in range(2):
                 total = ybuf[0, 3, h, ab] + r1[ab, 1, h] + r2[ab, h]
-                xg[me, h, ab] = (first_half_terms(h, ab) + total).astype(BF16).astype(F32)
+                xg[me, h, ab] = (residual(h, ab) + total).astype(BF16).astype(F32)
+            if h == 1 and before_last is not None:
+                before_last()
             for m in range(3):
                 ag_copy(m, h).start()
 
@@ -387,29 +410,35 @@
         wd_copy(t).start()
     add_partner(3)
     resid_copy.wait()
-    reduce_scatter_rest(lambda h, ab: resid_buf[h * half:(h + 1) * half, ab * piece:(ab + 1) * piece].astype(F32))
-
-    parts = []
-    for h in range(2):
-        sq = jnp.zeros((half, 1), F32)
-        for ab in range(2):
-            vals = xg[me, h, ab]
-            sq = sq + jnp.sum(vals * vals, axis=-1, keepdims=True)
-        parts.append(sq)
-    sq = jnp.concatenate(parts, axis=0)
-    stat_out[...] = jnp.transpose(jnp.broadcast_to(sq, (rows, 128)))[:8]
+    gain_copy.wait()
+    gbuf[...] = gain_buf[...].astype(F32)
 
     def st_copy(j):
         return remote(stat_out, stat.at[j], st_send.at[j], st_recv.at[j], (tp + j) % 8)
 
-    for j in range(1, 8):
-        st_copy(j).start()
-    sq_all = stat_out[...]
-    for j in range(1, 8):
-        st_copy(j).wait_recv()
-        sq_all = sq_all + stat[j]
-    scale = lax.rsqrt(sq_all * (1.0 / width) + EPS)
-    rbuf[...] = jnp.transpose(jnp.broadcast_to(scale[:1], (128, rows)))
+    def send_row_sums():
+        parts = []
+        for h in range(2):
+            sq = jnp.zeros((half, 1), F32)
+            for ab in range(2):
+                vals = xg[me, h, ab]
+                sq = sq + jnp.sum(vals * vals, axis=-1, keepdims=True)
+            parts.append(sq)
+        sq = jnp.concatenate(parts, axis=0)
+        stat_out[...] = jnp.transpose(jnp.broadcast_to(sq, (rows, 128)))[:8]
+        for j in range(1, 8):
+            st_copy(j).start()
+
+    def read_row_scales():
+        sq_all = stat_out[...]
+        for j in range(1, 8):
+            st_copy(j).wait_recv()
+            sq_all = sq_all + stat[j]
+        scale = lax.rsqrt(sq_all * (1.0 / width) + EPS)
+        rbuf[...] = jnp.transpose(jnp.broadcast_to(scale[:1], (128, rows)))
+
+    reduce_scatter_rest(lambda h, ab: resid_buf[h * half:(h + 1) * half, ab * piece:(ab + 1) * piece].astype(F32),
+                        send_row_sums)
 
     def gate_up(k):
         o = owner(*GATHER_ORDER[k])
@@ -436,11 +465,12 @@
             for copy in gu_copies(k + GU_SLOTS):
                 copy.start()
 
+    forward_first(0)
+    read_row_scales()
     gate_up(0)
     got(2, 0)
     got(2, 1)
     gate_up(1)
-    forward_first(0)
     forward_first(1)
     gate_up(2)
     gate_up(3)
@@ -476,16 +506,12 @@
     add_partner(3)
     reduce_scatter_rest(lambda h, ab: xg[me, h, ab])
 
-    def out_copy(k):
-        o = owner(*GATHER_ORDER[k])
-        return pltpu.make_async_copy(obuf.at[k], out_hbm.at[:, cols(o)], out_sem.at[k])
-
     def write_out(k):
         o = owner(*GATHER_ORDER[k])
         for h in range(2):
             for ab in range(2):
-                obuf[k, h * half:(h + 1) * half, ab * piece:(ab + 1) * piece] = xg[o, h, ab].astype(BF16)
-        out_copy(k).start()
+                out_ref[h * half:(h + 1) * half, pl.ds(pl.multiple_of(o * block + ab * piece, 128), piece)] = (
+                    xg[o, h, ab].astype(BF16))
 
     write_out(0)
     got(2, 0)
@@ -511,8 +537,6 @@
         st_copy(j).wait_send()
     wait_rs_sends()
     wait_ag_sends()
-    for k in range(8):
-        out_copy(k).wait()
 
 
 def mlp_tail(attn_out, resid_in, gain_mlp, w_out, w_gate, w_up, w_down):
@@ -525,9 +549,9 @@
     dma = pltpu.SemaphoreType.DMA
     return pl.pallas_call(
         tail_kernel,
-        out_shape=jax.ShapeDtypeStruct((rows, width), BF16),
-        in_specs=[pl.BlockSpec(memory_space=pltpu.VMEM)] * 2 + [pl.BlockSpec(memory_space=pl.ANY)] * 5,
-        out_specs=pl.BlockSpec(memory_space=pl.ANY),
+        out_shape=pltpu.VMEM((rows, width), BF16),
+        in_specs=[pl.BlockSpec(memory_space=pltpu.VMEM)] + [pl.BlockSpec(memory_space=pl.ANY)] * 6,
+        out_specs=pl.BlockSpec(memory_space=pltpu.VMEM),
         scratch_shapes=[
             pltpu.VMEM((WO_SLOTS, depth, block), BF16),
             pltpu.VMEM((GU_SLOTS, block, ffn), BF16),
@@ -543,16 +567,16 @@
             pltpu.VMEM((rows, ffn), BF16),
             pltpu.VMEM((rows, block), BF16),
             pltpu.VMEM((rows, block), BF16),
-            pltpu.VMEM((8, rows, block), BF16),
             pltpu.VMEM((8, 8, rows), F32),
             pltpu.VMEM((8, rows), F32),
+            pltpu.VMEM((width // 128, 128), BF16),
             pltpu.VMEM((width // 128, 128), F32),
             pltpu.VMEM((rows, 128), F32),
             dma((WO_SLOTS,)),
             dma((2, GU_SLOTS)),
             dma((WD_SLOTS,)),
             dma(()),
-            dma((8,)),
+            dma(()),
             dma((4,)),
             dma((4,)),
             dma((6, 2)),
@@ -563,8 +587,24 @@
             dma((8,)),
         ],
         compiler_params=pltpu.CompilerParams(collective_id=0, has_side_effects=True,
-                                             vmem_limit_bytes=67_000_000),
-    )(attn_out, gain_mlp.reshape(width // 128, 128), resid_in, w_out, w_gate, w_up, w_down)
+                                             vmem_limit_bytes=64_500_000),
+    )(in_vmem(attn_out), *map(in_hbm, (gain_mlp.reshape(width // 128, 128), resid_in, w_out, w_gate, w_up, w_down)))
+
+
+def write_kernel(resid_ref, resid_hbm, sem):
+    copy = pltpu.make_async_copy(resid_ref, resid_hbm, sem)
+    copy.start()
+    copy.wait()
+
+
+def write_back(resid_out):
+    return pl.pallas_call(
+        write_kernel,
+        out_shape=jax.ShapeDtypeStruct(resid_out.shape, resid_out.dtype),
+        in_specs=[pl.BlockSpec(memory_space=pltpu.VMEM)],
+        out_specs=pl.BlockSpec(memory_space=pl.ANY),
+        scratch_shapes=[pltpu.SemaphoreType.DMA(())],
+    )(in_vmem(resid_out))
 
 
 def solution(mesh):
@@ -573,7 +613,7 @@
         attn_out, k_full, v_full = attention(resid_in, positions, k_cache, v_cache, gain_attn,
                                              w_query, w_key, w_value)
         resid_out = mlp_tail(attn_out, resid_in, gain_mlp, w_out, w_gate, w_up, w_down)
-        return resid_out, k_full, v_full
+        return write_back(resid_out), k_full, v_full
 
     row_spec = P('dp', None)
     cache_spec = P('dp', None, 'tp', None)

time: 92.9 us -> 83.7 us (0.901)
  Pallas kernels: 88.2 us -> 82.7 us
  local copies, waits for them, and re-layouts: 2.69 us -> 0 us
    pallas_call x2 -> x3, Pallas kernels: 88.2 us -> 82.7 us  [the longest x1 68.4 us: mlp_tail(): pl.pallas_call(tail_kernel, out_shape=pltpu.VMEM((rows, width), BF16), in...]
    unnamed x1 -> x0, local copies, waits for them, and re-layouts: 2.69 us -> none
where the time goes in v3:
time: 83.7 us; the launch traced here: 83.5 us
  Pallas kernels  82.7 us (99%)
    pallas_call x1, Pallas kernels, mlp_tail(): pl.pallas_call(tail_kernel, out_shape=pltpu.VMEM((rows, width), BF16), in...  68.4 us
    pallas_call x1, Pallas kernels, attention(): pl.pallas_call(attention_kernel, out_shape=(pltpu.VMEM((rows, q_width), B...  13.2 us

profile of v3, /device:TPU:0, one launch (start us, length us, event | category | flops | bytes accessed | tf_op | source)
XLA Modules:
  0.0 83.5 jit_solution(15265940366670019724)
XLA Ops:
  0.6 13.2 %shard_map.157 = (bf16[128,768]{1,0:T(8,128)(2,1)S(1)}, bf16[128,128,128]{2,1,0:T(8,128)(2,1)}, bf16[128,128,128]{2,1,0:T(8,128)(2,1)}) custom-call(s32[128]{0:T(128)} %pos_hbm.1, s32[1,128]{1,0:T(1,128)} %bitcast.15, f32[1,128]{1,0:T(1,128)} %constant.2.clone.inv_hbm, bf16[48,128]{1,0:T(8,128)(2,1)} %bitcast.13, bf16[128,6144]{1,0:T(8,128)(2,1)} %resid_hbm.3, ...), custom_call_target="tpu_custom_call" | custom-call | tf_op jit(solution)/shard_map/pallas_call | solution.py:187
  13.8 68.4 %shard_map.158.resid_ref = bf16[128,6144]{1,0:T(8,128)(2,1)S(1)} custom-call(bf16[128,768]{1,0:T(8,128)(2,1)S(1)} %get-tuple-element.6.attn_ref, bf16[48,128]{1,0:T(8,128)(2,1)} %bitcast.14, bf16[128,6144]{1,0:T(8,128)(2,1)} %resid_hbm.3, bf16[768,6144]{1,0:T(8,128)(2,1)} %wo_hbm.1, bf16[6144,2048]{1,0:T(8,128)(2,1)} %wg_hbm.1, bf16[6144,2048]{1,0:T(8,128)(2,1)} %wu_hbm.1, ...), custom_call_target="tpu_custom_call" | custom-call | tf_op jit(solution)/shard_map/pallas_call | solution.py:550
  82.2 1.2 %shard_map.159 = bf16[128,6144]{1,0:T(8,128)(2,1)} custom-call(bf16[128,6144]{1,0:T(8,128)(2,1)S(1)} %shard_map.158.resid_ref), custom_call_target="tpu_custom_call" | custom-call | tf_op jit(solution)/shard_map/pallas_call | solution.py:601
